TPU v7x, 128 devices: a whole 4x4x4 slice. The times are simulated.
128 devices in a mesh: blk: 16 (over y, z), tm: 8 (over x, core).
Axes of the slice: x: 4, y: 4, z: 4, core: 2. Of those that a mesh axis runs over, the one named last changes fastest.
Arguments:
- solution: float32 [512, 128, 1024], P('blk', 'tm'), may hold values from -6 to 6
- residual: float32 [512, 128, 1024], P('blk', 'tm'), may hold values from -12 to 12
- direction: float32 [512, 128, 1024], P('blk', 'tm'), may hold values from -6 to 6
- noise_var: float32 [512, 128, 1024], P('blk', 'tm'), may hold values from 0.5 to 2
- legendre: bfloat16 [512, 512, 512], P('blk', 'tm'), may hold values from -0.25 to 0.25
- temporal: float32 [512, 128, 128], P('tm'), may hold values from -3 to 3.5, as said below
- order_table: int32 [512], replicated, may hold values from 0 to 511, as said below
Outputs:
- solution_new: float32 [512, 128, 1024], P('blk', 'tm')
- residual_new: float32 [512, 128, 1024], P('blk', 'tm')
- direction_new: float32 [512, 128, 1024], P('blk', 'tm')
Inputs may be any that keep to these rules, and one draw needn't show every extreme that they name: `order_table`: each value 0 to 511 appears once. In each aligned block of 32 entries, entry 16 + k equals 511 minus entry k, so each block holds pairs of orders m and 511 - m. `temporal`: each matrix is symmetric and positive definite.
All inputs are finite; a program needn't handle non-finite values.
Results may differ from a plain program's by a relative error of at most 0.0048.
Values may be sent and summed in bfloat16 or wider, within the bound.
A program may use at most 192 MiB of HBM per device.

v0:
```python
import math
import jax
import jax.numpy as jnp
from jax import lax
from jax.sharding import Mesh
from jax.sharding import PartitionSpec as P

BLK = ("blk_0", "blk_1")
TM = ("tm_0", "tm_1")
BLK_TM = ("blk_0", "blk_1", "tm_0", "tm_1")


def trig_table(orders, length):
    points = jnp.arange(128, dtype=jnp.int32)
    step = 2.0 * math.pi / length
    scale = 1.0 / math.sqrt(length / 2.0)
    fine = (orders[:, None] * points[None, :] % length).astype(jnp.float32) * step
    cos_fine, sin_fine = (jnp.cos(fine) * scale, jnp.sin(fine) * scale)
    coarse = jnp.arange(length // 128, dtype=jnp.int32) * 128
    shift = (orders[:, None] * coarse[None, :] % length).astype(jnp.float32) * step
    cos_shift, sin_shift = (jnp.cos(shift), jnp.sin(shift))
    cos_parts, sin_parts = ([], [])
    for q in range(length // 128):
        a, b = (cos_shift[:, q : q + 1], sin_shift[:, q : q + 1])
        cos_parts.append((cos_fine * a - sin_fine * b).astype(jnp.bfloat16))
        sin_parts.append((sin_fine * a + cos_fine * b).astype(jnp.bfloat16))
    return (jnp.concatenate(cos_parts, axis=1), jnp.concatenate(sin_parts, axis=1))


def body(solution, residual, direction, noise_var, legendre, temporal, order_table):
    per_device, deg_dev, lat_all = legendre.shape
    lat_dev, time_dev, longitude = direction.shape
    blocks = lat_all // lat_dev
    cos_table, sin_table = trig_table(order_table, longitude)
    table = jnp.stack(
        [
            cos_table.reshape(blocks, per_device, longitude),
            sin_table.reshape(blocks, per_device, longitude),
        ],
        axis=1,
    )
    own_orders = lax.dynamic_slice_in_dim(order_table, lax.axis_index(BLK) * per_device, per_device)
    own_degrees = lax.axis_index(TM) * deg_dev + jnp.arange(deg_dev, dtype=jnp.int32)
    keep_mask = own_degrees[None, :, None] >= own_orders[:, None, None]
    masked = jnp.where(keep_mask, legendre, jnp.zeros_like(legendre))
    flat = table.reshape(-1, longitude)
    spectra = jnp.einsum(
        "kj,atj->kta", flat, direction.astype(jnp.bfloat16), preferred_element_type=jnp.float32
    ).astype(jnp.bfloat16)
    cycles = lax.all_to_all(
        spectra.reshape(blocks, 2 * per_device * time_dev * lat_dev),
        BLK,
        split_axis=0,
        concat_axis=0,
        tiled=True,
    )
    cycles = cycles.reshape(blocks, 2, per_device, time_dev, lat_dev)
    cycles = cycles.transpose(2, 1, 3, 0, 4).reshape(per_device, 2, time_dev, lat_all)
    cycles = lax.all_gather(cycles, TM, axis=2, tiled=True)
    coeffs = jnp.einsum(
        "icta,ila->lict", cycles, masked, preferred_element_type=jnp.float32
    ).astype(jnp.bfloat16)
    mixed = jnp.einsum(
        "lict,ltu->licu", coeffs, temporal.astype(jnp.bfloat16), preferred_element_type=jnp.float32
    ).astype(jnp.bfloat16)
    terms = jnp.einsum("ila,licu->icua", masked, mixed, preferred_element_type=jnp.float32).astype(
        jnp.bfloat16
    )
    terms = lax.psum_scatter(terms, TM, scatter_dimension=2, tiled=True)
    terms = terms.reshape(per_device, 2, time_dev, blocks, lat_dev).transpose(3, 1, 0, 2, 4)
    entries = lax.all_to_all(
        terms.reshape(blocks, -1), BLK, split_axis=0, concat_axis=0, tiled=True
    )
    entries = entries.reshape(blocks * 2 * per_device, time_dev, lat_dev)
    synthesis = jnp.einsum("kta,kj->atj", entries, flat, preferred_element_type=jnp.float32)
    product = synthesis + noise_var * direction
    sums = jnp.stack(
        [
            jnp.sum(residual * residual),
            jnp.sum(direction * product),
            jnp.sum(residual * product),
            jnp.sum(product * product),
        ]
    )
    norm_now, curvature, cross, square = lax.psum(sums, BLK_TM)
    step_size = norm_now / curvature
    norm_next = norm_now - 2.0 * step_size * cross + step_size * step_size * square
    residual_new = residual - step_size * product
    return (
        solution + step_size * direction,
        residual_new,
        residual_new + norm_next / norm_now * direction,
    )


def solution(mesh):
    torus = Mesh(mesh.devices.reshape(4, 4, 4, 2), ("blk_0", "blk_1", "tm_0", "tm_1"))
    return jax.shard_map(
        body,
        mesh=torus,
        in_specs=(
            P(BLK, TM, None),
            P(BLK, TM, None),
            P(BLK, TM, None),
            P(BLK, TM, None),
            P(BLK, TM, None),
            P(TM, None, None),
            P(),
        ),
        out_specs=(P(BLK, TM, None), P(BLK, TM, None), P(BLK, TM, None)),
        check_vma=False,
    )
```

profile of v0, /device:TPU:1, one launch (start us, length us, event | category | flops | bytes accessed | tf_op | source)
XLA Modules:
  0.0 380.3 jit_solution(8376682952619648902)
XLA Ops:
  10.2 1.8 convert_element_type.275
  24.7 1.5 fusion.13
  26.1 4.8 %copy.39 = bf16[1024,16,32]{2,1,0:T(8,128)(2,1)} copy(bf16[1024,16,32]{0,2,1:T(8,128)(2,1)S(1)} %fusion.13) | data formatting | bytes 2097152 | tf_op jit(solution)/shard_map/convert_element_type | solution.py:49
  30.9 6.3 %all_to_all.16 = bf16[16,1,32768]{2,1,0:T(2,128)(2,1)S(1)} reshape(bf16[1024,16,32]{2,1,0:T(8,128)(2,1)} %copy.39) | data formatting | bytes 2097152 | tf_op jit(solution)/shard_map/all_to_all | solution.py:50
  37.7 7.0 %reduce.66 = bf16[16,32768]{1,0:T(8,128)(2,1)S(1)} reduce(bf16[16,1,32768]{2,1,0:T(2,128)(2,1)S(1)} %all_to_all.16, bf16[]{:T(256)} %broadcast.1093), dimensions={1}, to_apply=%all_to_all.16.reduce_sub_computation | reduce | bytes 2097154 | tf_op jit(solution)/shard_map/all_to_all | solution.py:50
  45.6 24.6 %all_to_all.20 = bf16[16,2,16384]{2,1,0:T(2,128)(2,1)S(1)} all-to-all(bf16[16,2,16384]{2,1,0:T(2,128)(2,1)S(1)} %reshape.811), channel_id=1, replica_groups=mesh['blk_0'=4,'blk_1'=4,'tm_0'=4,'tm_1'=2] {'blk_0','blk_1'}, dimensions={0} | all-to-all | bytes 2097152 | tf_op jit(solution)/shard_map/all_to_all | solution.py:50
  71.2 6.4 %reduce.16 = bf16[16,32768]{1,0:T(8,128)(2,1)S(1)} reduce(bf16[16,1,32768]{2,1,0:T(2,128)(2,1)S(1)} %reshape.812, bf16[]{:T(256)} %constant.78), dimensions={1}, to_apply=%all_to_all.13.reduce_sub_computation | reduce | bytes 2097154 | tf_op jit(solution)/shard_map/all_to_all | solution.py:50
  77.6 5.0 %reshape.718 = bf16[16,2,32,16,32]{4,3,2,1,0:T(8,128)(2,1)} reshape(bf16[16,32768]{1,0:T(8,128)(2,1)S(1)} %reduce.16) | data formatting | bytes 2097152 | tf_op jit(solution)/shard_map/reshape | solution.py:57
  82.6 9.0 %copy.41 = bf16[32,2,16,16,32]{4,3,2,1,0:T(8,128)(2,1)} copy(bf16[32,2,16,16,32]{4,2,0,1,3:T(8,128)(2,1)} %bitcast.51) | data formatting | bytes 2097152 | tf_op jit(solution)/shard_map/transpose | solution.py:58
  91.6 6.9 %reshape.719 = bf16[32,2,16,512]{3,2,1,0:T(8,128)(2,1)} reshape(bf16[32,2,16,16,32]{4,3,2,1,0:T(8,128)(2,1)} %copy.41) | data formatting | bytes 2097152 | tf_op jit(solution)/shard_map/reshape | solution.py:58
  99.5 48.7 %all-gather.2.cloned.1.call-done = bf16[32,2,128,512]{3,2,1,0:T(8,128)(2,1)} async-done(((bf16[32,2,16,512]{3,2,1,0:T(8,128)(2,1)}), bf16[32,2,128,512]{3,2,1,0:T(8,128)(2,1)}) %all-gather.2.cloned.1.call-update) | async-done | bytes 8388624 | tf_op jit(solution)/shard_map/all_gather | solution.py:59
  148.2 6.2 %fusion.14 = bf16[64,32,2,128]{3,0,2,1:T(8,128)(2,1)S(1)} fusion(bf16[32,2,128,512]{3,2,1,0:T(8,128)(2,1)} %all-gather.2.cloned.1.call-done, bf16[32,64,512]{2,1,0:T(8,128)(2,1)S(1)} %copy-done.3, pred[32,64]{1,0:T(8,128)(4,1)S(1)} %broadcast_compare_fusion), kind=kOutput, calls=%fused_computation.23 | convolution fusion | flops 538443776 | bytes 11536384 | tf_op jit(solution)/shard_map/icta,ila->lict/dot_general | solution.py:60
  155.7 4.9 %convolution_convert_fusion = bf16[32,2,128,512]{3,2,1,0:T(8,128)(2,1)} fusion(bf16[32,64,512]{2,1,0:T(8,128)(2,1)S(1)} %copy-done.3, pred[32,64]{1,0:T(8,128)(4,1)S(1)} %broadcast_compare_fusion, bf16[64,32,2,128]{3,1,2,0:T(8,128)(2,1)S(1)} %fusion.10), kind=kOutput, calls=%fused_computation | convolution fusion | flops 542113792 | bytes 11536384 | tf_op jit(solution)/shard_map/ila,licu->icua/dot_general | solution.py:66
  160.6 51.8 %reduce-scatter.2.cloned.1.call-done = bf16[32,2,16,512]{3,2,1,0:T(8,128)(2,1)} async-done(((bf16[32,2,128,512]{3,2,1,0:T(8,128)(2,1)}), bf16[32,2,16,512]{3,2,1,0:T(8,128)(2,1)}) %reduce-scatter.2.cloned.1.call-update) | async-done | bytes 1048592 | tf_op jit(solution)/shard_map/reduce_scatter | solution.py:69
  212.4 5.9 %reshape.720 = bf16[32,2,16,16,32]{4,3,2,1,0:T(8,128)(2,1)} reshape(bf16[32,2,16,512]{3,2,1,0:T(8,128)(2,1)} %reduce-scatter.2.cloned.1.call-done) | data formatting | bytes 2097152 | tf_op jit(solution)/shard_map/reshape | solution.py:70
  218.3 5.2 %copy.80 = bf16[32,2,16,16,32]{4,2,0,1,3:T(8,128)(2,1)} copy(bf16[32,2,16,16,32]{4,3,2,1,0:T(8,128)(2,1)} %reshape.720) | data formatting | bytes 2097152 | tf_op jit(solution)/shard_map/reshape | solution.py:70
  223.6 6.1 %all_to_all.17 = bf16[16,1,32768]{2,1,0:T(2,128)(2,1)S(1)} reshape(bf16[16,2,32,16,32]{4,3,2,1,0:T(8,128)(2,1)} %bitcast.52) | data formatting | bytes 2097152 | tf_op jit(solution)/shard_map/all_to_all | solution.py:71
  229.6 7.0 %reduce.67 = bf16[16,32768]{1,0:T(8,128)(2,1)S(1)} reduce(bf16[16,1,32768]{2,1,0:T(2,128)(2,1)S(1)} %all_to_all.17, bf16[]{:T(256)} %broadcast.1093), dimensions={1}, to_apply=%all_to_all.17.reduce_sub_computation | reduce | bytes 2097154 | tf_op jit(solution)/shard_map/all_to_all | solution.py:71
  236.7 1.6 reshape.813
  238.2 6.9 %all-to-all-start.1 = ((bf16[16,2,16384]{2,1,0:T(2,128)(2,1)}), bf16[16,2,16384]{2,1,0:T(2,128)(2,1)S(1)}, u32[]{:S(2)}, u32[]{:S(2)}) async-start(bf16[16,2,16384]{2,1,0:T(2,128)(2,1)} %reshape.813), calls=%async_computation.2 | async-start | bytes 2097152 | tf_op jit(solution)/shard_map/all_to_all | solution.py:71
  246.3 14.2 %all-to-all-done.1 = bf16[16,2,16384]{2,1,0:T(2,128)(2,1)S(1)} async-done(((bf16[16,2,16384]{2,1,0:T(2,128)(2,1)}), bf16[16,2,16384]{2,1,0:T(2,128)(2,1)S(1)}, u32[]{:S(2)}, u32[]{:S(2)}) %all-to-all-start.1) | async-done | bytes 1048608 | tf_op jit(solution)/shard_map/all_to_all | solution.py:71
  261.6 6.4 %reduce.17 = bf16[16,32768]{1,0:T(8,128)(2,1)S(1)} reduce(bf16[16,1,32768]{2,1,0:T(2,128)(2,1)S(1)} %reshape.814, bf16[]{:T(256)} %constant.78), dimensions={1}, to_apply=%all_to_all.15.reduce_sub_computation | reduce | bytes 2097154 | tf_op jit(solution)/shard_map/all_to_all | solution.py:71
  267.9 4.6 %reshape.721 = bf16[1024,16,32]{2,1,0:T(8,128)(2,1)} reshape(bf16[16,32768]{1,0:T(8,128)(2,1)S(1)} %reduce.17) | data formatting | bytes 2097152 | tf_op jit(solution)/shard_map/reshape | solution.py:74
  272.5 4.7 %copy.46 = bf16[1024,16,32]{0,2,1:T(8,128)(2,1)S(1)} copy(bf16[1024,16,32]{2,1,0:T(8,128)(2,1)} %reshape.721) | data formatting | bytes 2097152 | tf_op jit(solution)/shard_map/reshape | solution.py:74
  277.2 3.0 fusion.71
  280.7 5.6 %multiply_reduce_fusion.2 = (f32[]{:T(128)}, f32[]{:T(128)}, f32[]{:T(128)}, f32[32,16,1024]{2,0,1:T(8,128)}) fusion(f32[32,16,1024]{2,1,0:T(8,128)S(1)} %copy-done, f32[32,16,1024]{2,1,0:T(8,128)S(1)} %copy-done.2, f32[32,16,1024]{2,0,1:T(8,128)S(1)} %bitcast.55, f32[32,16,1024]{2,1,0:T(8,128)S(1)} %copy-done.6), kind=kLoop, calls=%fused_computation.15 | loop fusion | flops 4194301 | bytes 10485772 | tf_op jit(solution)/shard_map/reduce_sum | solution.py:80
  286.3 2.7 pad_maximum_fusion.1
  289.0 65.2 %psum.7 = f32[4]{0:T(128)S(1)} all-reduce(f32[4]{0:T(128)S(1)} %pad_maximum_fusion.1), channel_id=1, replica_groups=mesh['blk_0'=4,'blk_1'=4,'tm_0'=4,'tm_1'=2] {'blk_0','blk_1','tm_0','tm_1'}, use_global_device_ids=true, to_apply=%region_5.6 | all-reduce | flops 4 | bytes 32 | tf_op jit(solution)/shard_map/psum | solution.py:85
  358.6 6.8 %multiply_add_fusion = (f32[32,16,1024]{2,0,1:T(8,128)S(1)}, f32[32,16,1024]{2,0,1:T(8,128)S(1)}, f32[32,16,1024]{2,0,1:T(8,128)S(1)}) fusion(f32[32,16,1024]{2,1,0:T(8,128)S(1)} %copy-done, f32[]{:T(128)S(6)} %div.7, f32[32,16,1024]{2,0,1:T(8,128)} %get-tuple-element.33, f32[]{:T(128)S(6)} %div.6, f32[32,16,1024]{2,1,0:T(8,128)} %param.8, ...), kind=kLoop, calls=%fused_computation.11 | loop fusion | flops 3145728 | bytes 14680072 | tf_op jit(solution)/shard_map/add | solution.py:92
  365.4 2.5 copy.55
  367.9 2.5 copy.56
  370.5 2.5 copy.57
  (57 shorter events, 23.5 us)
Async XLA Ops:
  7.2 141.0 %all-gather.2.cloned.1.call-start = ((), (), s32[]{:S(2)}) async-start(), calls=%async_computation.3 | async-start | bytes 9437184 | tf_op jit(solution)/shard_map/all_gather | solution.py:59
  23.4 1.3 copy-start.5
  91.6 56.6 %copy-start.3 = (bf16[32,64,512]{2,1,0:T(8,128)(2,1)S(1)}, bf16[32,64,512]{2,1,0:T(8,128)(2,1)}, u32[]{:S(2)}) copy-start(bf16[32,64,512]{2,1,0:T(8,128)(2,1)} %param.11) | copy-start | bytes 6291460
  98.6 113.8 %reduce-scatter.2.cloned.1.call-start = ((), (), s32[]{:S(2)}) async-start(), calls=%async_computation.4 | async-start | bytes 9437184 | tf_op jit(solution)/shard_map/reduce_scatter | solution.py:69
  148.2 6.2 %copy-start.4 = (f32[64,128,128]{2,1,0:T(8,128)S(1)}, f32[64,128,128]{2,1,0:T(8,128)}, u32[]{:S(2)}) copy-start(f32[64,128,128]{2,1,0:T(8,128)} %param.12) | copy-start | bytes 12582916
  236.6 8.5 %copy-start.1 = (f32[32,16,1024]{2,1,0:T(8,128)S(1)}, f32[32,16,1024]{2,1,0:T(8,128)}, u32[]{:S(2)}) copy-start(f32[32,16,1024]{2,1,0:T(8,128)} %param.8) | copy-start | bytes 6291460
  238.2 22.3 %all-to-all-start.1 = ((bf16[16,2,16384]{2,1,0:T(2,128)(2,1)}), bf16[16,2,16384]{2,1,0:T(2,128)(2,1)S(1)}, u32[]{:S(2)}, u32[]{:S(2)}) async-start(bf16[16,2,16384]{2,1,0:T(2,128)(2,1)} %reshape.813), calls=%async_computation.2 | async-start | bytes 2097152 | tf_op jit(solution)/shard_map/all_to_all | solution.py:71
  277.2 3.0 copy-start
  277.2 3.0 copy-start.2
  277.2 3.5 copy-start.6
Sparse Core Ops, SparseCore 0:
  98.7 49.4 all-gather.1
  160.7 51.6 reduce-scatter.1
where the time goes:
time: 387 us; the launch traced here: 380 us
  waiting for transfers between devices  115 us (30%)
  blocking collectives  89.8 us (23%)
  local copies, waits for them, and re-layouts  76.3 us (20%)
  other arithmetic  57.2 us (15%)
  between operations  18.5 us (5%)
  matrix products  16.8 us (4%)
  starting transfers between devices  7 us (2%)
    psum x1, blocking collectives, body(): norm_now, curvature, cross, square = lax.psum(sums, BLK_TM)  65.2 us
    reduce_scatter x1, waiting for transfers between devices, body(): terms = lax.psum_scatter(terms, TM, scatter_dimension=2, tiled=True)  51.8 us
    all_gather x1, waiting for transfers between devices, body(): cycles = lax.all_gather(cycles, TM, axis=2, tiled=True)  48.7 us
    all_to_all x1, blocking collectives, body(): lax.all_to_all(spectra.reshape(blocks, 2 * per_device * time_dev * lat_de...  24.6 us
    all_to_all x1, waiting for transfers between devices, body(): lax.all_to_all(terms.reshape(blocks, -1), BLK, split_axis=0, concat_axis=...  14.2 us
    unnamed x21, local copies, waits for them, and re-layouts  13.9 us
    all_to_all x2, other arithmetic, body(): lax.all_to_all(terms.reshape(blocks, -1), BLK, split_axis=0, concat_axis=...  13.4 us
    all_to_all x2, other arithmetic, body(): lax.all_to_all(spectra.reshape(blocks, 2 * per_device * time_dev * lat_de...  13.4 us
  transfers between devices with their start and end apart: 3, of which 3 were waited for; matrix products, arithmetic and copies ran while one was open for 1% of the time, Pallas kernels for 0%

commit v1 on v0

--- a/solution.py
+++ b/solution.py
@@ -8,6 +8,12 @@
 BLK = ("blk_0", "blk_1")
 TM = ("tm_0", "tm_1")
 BLK_TM = ("blk_0", "blk_1", "tm_0", "tm_1")
+
+
+def add_all(shard, axis):
+    parts = lax.all_gather(shard, axis, axis=0, tiled=False)
+    total = parts.sum(axis=0)
+    return total
 
 
 def trig_table(orders, length):
@@ -82,7 +88,7 @@
             jnp.sum(product * product),
         ]
     )
-    norm_now, curvature, cross, square = lax.psum(sums, BLK_TM)
+    norm_now, curvature, cross, square = add_all(sums, BLK_TM)
     step_size = norm_now / curvature
     norm_next = norm_now - 2.0 * step_size * cross + step_size * step_size * square
     residual_new = residual - step_size * product

time: 387 us -> 388 us (level)
    unnamed x0 -> x1, blocking collectives: none -> 65.4 us
    psum x1 -> x0, blocking collectives: 65.2 us -> none  [body(): norm_now, curvature, cross, square = lax.psum(sums, BLK_TM)]
    unnamed x7 -> x8, other arithmetic: 9.75 us -> 12.5 us
    unnamed x21 -> x22, local copies, waits for them, and re-layouts: 13.9 us -> 13.9 us
where the time goes in v1:
time: 388 us; the launch traced here: 381 us
  waiting for transfers between devices  115 us (30%)
  blocking collectives  90 us (23%)
  local copies, waits for them, and re-layouts  76.2 us (20%)
  other arithmetic  57.3 us (15%)
  between operations  18.5 us (5%)
  matrix products  16.8 us (4%)
  starting transfers between devices  7 us (2%)
    unnamed x1, blocking collectives  65.4 us
    reduce_scatter x1, waiting for transfers between devices, body(): terms = lax.psum_scatter(terms, TM, scatter_dimension=2, tiled=True)  51.8 us
    all_gather x1, waiting for transfers between devices, body(): cycles = lax.all_gather(cycles, TM, axis=2, tiled=True)  48.7 us
    all_to_all x1, blocking collectives, body(): lax.all_to_all(spectra.reshape(blocks, 2 * per_device * time_dev * lat_de...  24.6 us
    all_to_all x1, waiting for transfers between devices, body(): lax.all_to_all(terms.reshape(blocks, -1), BLK, split_axis=0, concat_axis=...  14.2 us
    unnamed x22, local copies, waits for them, and re-layouts  13.9 us
    all_to_all x2, other arithmetic, body(): lax.all_to_all(terms.reshape(blocks, -1), BLK, split_axis=0, concat_axis=...  13.4 us
    all_to_all x2, other arithmetic, body(): lax.all_to_all(spectra.reshape(blocks, 2 * per_device * time_dev * lat_de...  13.4 us
  transfers between devices with their start and end apart: 3, of which 3 were waited for; matrix products, arithmetic and copies ran while one was open for 1% of the time, Pallas kernels for 0%

profile of v1, /device:TPU:1, one launch (start us, length us, event | category | flops | bytes accessed | tf_op | source)
XLA Modules:
  0.0 380.5 jit_solution(508148013894742451)
XLA Ops:
  10.2 1.8 convert_element_type.275
  24.7 1.5 fusion.13
  26.1 4.8 %copy.39 = bf16[1024,16,32]{2,1,0:T(8,128)(2,1)} copy(bf16[1024,16,32]{0,2,1:T(8,128)(2,1)S(1)} %fusion.13) | data formatting | bytes 2097152 | tf_op jit(solution)/shard_map/convert_element_type | solution.py:55
  30.9 6.3 %all_to_all.16 = bf16[16,1,32768]{2,1,0:T(2,128)(2,1)S(1)} reshape(bf16[1024,16,32]{2,1,0:T(8,128)(2,1)} %copy.39) | data formatting | bytes 2097152 | tf_op jit(solution)/shard_map/all_to_all | solution.py:56
  37.7 7.0 %reduce.66 = bf16[16,32768]{1,0:T(8,128)(2,1)S(1)} reduce(bf16[16,1,32768]{2,1,0:T(2,128)(2,1)S(1)} %all_to_all.16, bf16[]{:T(256)} %broadcast.1094), dimensions={1}, to_apply=%all_to_all.16.reduce_sub_computation | reduce | bytes 2097154 | tf_op jit(solution)/shard_map/all_to_all | solution.py:56
  45.6 24.6 %all_to_all.20 = bf16[16,2,16384]{2,1,0:T(2,128)(2,1)S(1)} all-to-all(bf16[16,2,16384]{2,1,0:T(2,128)(2,1)S(1)} %reshape.814), channel_id=1, replica_groups=mesh['blk_0'=4,'blk_1'=4,'tm_0'=4,'tm_1'=2] {'blk_0','blk_1'}, dimensions={0} | all-to-all | bytes 2097152 | tf_op jit(solution)/shard_map/all_to_all | solution.py:56
  71.2 6.4 %reduce.16 = bf16[16,32768]{1,0:T(8,128)(2,1)S(1)} reduce(bf16[16,1,32768]{2,1,0:T(2,128)(2,1)S(1)} %reshape.815, bf16[]{:T(256)} %constant.82), dimensions={1}, to_apply=%all_to_all.13.reduce_sub_computation | reduce | bytes 2097154 | tf_op jit(solution)/shard_map/all_to_all | solution.py:56
  77.6 5.0 %reshape.718 = bf16[16,2,32,16,32]{4,3,2,1,0:T(8,128)(2,1)} reshape(bf16[16,32768]{1,0:T(8,128)(2,1)S(1)} %reduce.16) | data formatting | bytes 2097152 | tf_op jit(solution)/shard_map/reshape | solution.py:63
  82.6 9.0 %copy.41 = bf16[32,2,16,16,32]{4,3,2,1,0:T(8,128)(2,1)} copy(bf16[32,2,16,16,32]{4,2,0,1,3:T(8,128)(2,1)} %bitcast.51) | data formatting | bytes 2097152 | tf_op jit(solution)/shard_map/transpose | solution.py:64
  91.6 6.9 %reshape.719 = bf16[32,2,16,512]{3,2,1,0:T(8,128)(2,1)} reshape(bf16[32,2,16,16,32]{4,3,2,1,0:T(8,128)(2,1)} %copy.41) | data formatting | bytes 2097152 | tf_op jit(solution)/shard_map/reshape | solution.py:64
  99.5 48.7 %all-gather.3.cloned.1.call-done = bf16[32,2,128,512]{3,2,1,0:T(8,128)(2,1)} async-done(((bf16[32,2,16,512]{3,2,1,0:T(8,128)(2,1)}), bf16[32,2,128,512]{3,2,1,0:T(8,128)(2,1)}) %all-gather.3.cloned.1.call-update) | async-done | bytes 8388624 | tf_op jit(solution)/shard_map/all_gather | solution.py:65
  148.2 6.2 %fusion.14 = bf16[64,32,2,128]{3,0,2,1:T(8,128)(2,1)S(1)} fusion(bf16[32,2,128,512]{3,2,1,0:T(8,128)(2,1)} %all-gather.3.cloned.1.call-done, bf16[32,64,512]{2,1,0:T(8,128)(2,1)S(1)} %copy-done.3, pred[32,64]{1,0:T(8,128)(4,1)S(1)} %broadcast_compare_fusion), kind=kOutput, calls=%fused_computation.23 | convolution fusion | flops 538443776 | bytes 11536384 | tf_op jit(solution)/shard_map/icta,ila->lict/dot_general | solution.py:66
  155.7 4.9 %convolution_convert_fusion = bf16[32,2,128,512]{3,2,1,0:T(8,128)(2,1)} fusion(bf16[32,64,512]{2,1,0:T(8,128)(2,1)S(1)} %copy-done.3, pred[32,64]{1,0:T(8,128)(4,1)S(1)} %broadcast_compare_fusion, bf16[64,32,2,128]{3,1,2,0:T(8,128)(2,1)S(1)} %fusion.10), kind=kOutput, calls=%fused_computation | convolution fusion | flops 542113792 | bytes 11536384 | tf_op jit(solution)/shard_map/ila,licu->icua/dot_general | solution.py:72
  160.6 51.8 %reduce-scatter.2.cloned.1.call-done = bf16[32,2,16,512]{3,2,1,0:T(8,128)(2,1)} async-done(((bf16[32,2,128,512]{3,2,1,0:T(8,128)(2,1)}), bf16[32,2,16,512]{3,2,1,0:T(8,128)(2,1)}) %reduce-scatter.2.cloned.1.call-update) | async-done | bytes 1048592 | tf_op jit(solution)/shard_map/reduce_scatter | solution.py:75
  212.4 5.9 %reshape.720 = bf16[32,2,16,16,32]{4,3,2,1,0:T(8,128)(2,1)} reshape(bf16[32,2,16,512]{3,2,1,0:T(8,128)(2,1)} %reduce-scatter.2.cloned.1.call-done) | data formatting | bytes 2097152 | tf_op jit(solution)/shard_map/reshape | solution.py:76
  218.3 5.2 %copy.80 = bf16[32,2,16,16,32]{4,2,0,1,3:T(8,128)(2,1)} copy(bf16[32,2,16,16,32]{4,3,2,1,0:T(8,128)(2,1)} %reshape.720) | data formatting | bytes 2097152 | tf_op jit(solution)/shard_map/reshape | solution.py:76
  223.6 6.1 %all_to_all.17 = bf16[16,1,32768]{2,1,0:T(2,128)(2,1)S(1)} reshape(bf16[16,2,32,16,32]{4,3,2,1,0:T(8,128)(2,1)} %bitcast.52) | data formatting | bytes 2097152 | tf_op jit(solution)/shard_map/all_to_all | solution.py:77
  229.6 7.0 %reduce.67 = bf16[16,32768]{1,0:T(8,128)(2,1)S(1)} reduce(bf16[16,1,32768]{2,1,0:T(2,128)(2,1)S(1)} %all_to_all.17, bf16[]{:T(256)} %broadcast.1094), dimensions={1}, to_apply=%all_to_all.17.reduce_sub_computation | reduce | bytes 2097154 | tf_op jit(solution)/shard_map/all_to_all | solution.py:77
  236.7 1.6 reshape.816
  238.2 6.9 %all-to-all-start.1 = ((bf16[16,2,16384]{2,1,0:T(2,128)(2,1)}), bf16[16,2,16384]{2,1,0:T(2,128)(2,1)S(1)}, u32[]{:S(2)}, u32[]{:S(2)}) async-start(bf16[16,2,16384]{2,1,0:T(2,128)(2,1)} %reshape.816), calls=%async_computation.2 | async-start | bytes 2097152 | tf_op jit(solution)/shard_map/all_to_all | solution.py:77
  246.3 14.2 %all-to-all-done.1 = bf16[16,2,16384]{2,1,0:T(2,128)(2,1)S(1)} async-done(((bf16[16,2,16384]{2,1,0:T(2,128)(2,1)}), bf16[16,2,16384]{2,1,0:T(2,128)(2,1)S(1)}, u32[]{:S(2)}, u32[]{:S(2)}) %all-to-all-start.1) | async-done | bytes 1048608 | tf_op jit(solution)/shard_map/all_to_all | solution.py:77
  261.6 6.4 %reduce.17 = bf16[16,32768]{1,0:T(8,128)(2,1)S(1)} reduce(bf16[16,1,32768]{2,1,0:T(2,128)(2,1)S(1)} %reshape.817, bf16[]{:T(256)} %constant.82), dimensions={1}, to_apply=%all_to_all.15.reduce_sub_computation | reduce | bytes 2097154 | tf_op jit(solution)/shard_map/all_to_all | solution.py:77
  267.9 4.6 %reshape.721 = bf16[1024,16,32]{2,1,0:T(8,128)(2,1)} reshape(bf16[16,32768]{1,0:T(8,128)(2,1)S(1)} %reduce.17) | data formatting | bytes 2097152 | tf_op jit(solution)/shard_map/reshape | solution.py:80
  272.5 4.4 %copy.46 = bf16[1024,16,32]{0,2,1:T(8,128)(2,1)S(1)} copy(bf16[1024,16,32]{2,1,0:T(8,128)(2,1)} %reshape.721) | data formatting | bytes 2097152 | tf_op jit(solution)/shard_map/reshape | solution.py:80
  277.0 3.0 fusion.71
  280.5 5.6 %multiply_reduce_fusion.2 = (f32[]{:T(128)}, f32[]{:T(128)}, f32[]{:T(128)}, f32[32,16,1024]{2,0,1:T(8,128)}) fusion(f32[32,16,1024]{2,1,0:T(8,128)S(1)} %copy-done, f32[32,16,1024]{2,1,0:T(8,128)S(1)} %copy-done.2, f32[32,16,1024]{2,0,1:T(8,128)S(1)} %bitcast.55, f32[32,16,1024]{2,1,0:T(8,128)S(1)} %copy-done.6), kind=kLoop, calls=%fused_computation.15 | loop fusion | flops 4194301 | bytes 10485772 | tf_op jit(solution)/shard_map/reduce_sum | solution.py:86
  286.1 2.8 maximum_dynamic-update-slice_fusion
  288.9 65.4 %all-reduce = f32[512]{0:T(512)S(1)} all-reduce(f32[512]{0:T(512)S(1)} %maximum_dynamic-update-slice_fusion), channel_id=2, replica_groups=mesh['blk_0'=4,'blk_1'=4,'tm_0'=4,'tm_1'=2] {'blk_0','blk_1','tm_0','tm_1'}, use_global_device_ids=true, to_apply=%add | all-reduce | flops 512 | bytes 4096
  358.9 6.8 %multiply_add_fusion = (f32[32,16,1024]{2,0,1:T(8,128)S(1)}, f32[32,16,1024]{2,0,1:T(8,128)S(1)}, f32[32,16,1024]{2,0,1:T(8,128)S(1)}) fusion(f32[32,16,1024]{2,1,0:T(8,128)S(1)} %copy-done, f32[]{:T(128)S(6)} %div.7, f32[32,16,1024]{2,0,1:T(8,128)} %get-tuple-element.33, f32[]{:T(128)S(6)} %div.6, f32[32,16,1024]{2,1,0:T(8,128)} %param.8, ...), kind=kLoop, calls=%fused_computation.11 | loop fusion | flops 3145728 | bytes 14680072 | tf_op jit(solution)/shard_map/add | solution.py:98
  365.7 2.5 copy.55
  368.2 2.5 copy.56
  370.7 2.5 copy.57
  (60 shorter events, 23.6 us)
Async XLA Ops:
  7.2 141.0 %all-gather.3.cloned.1.call-start = ((), (), s32[]{:S(2)}) async-start(), calls=%async_computation.3 | async-start | bytes 9437184 | tf_op jit(solution)/shard_map/all_gather | solution.py:65
  23.4 1.3 copy-start.5
  91.6 56.6 %copy-start.3 = (bf16[32,64,512]{2,1,0:T(8,128)(2,1)S(1)}, bf16[32,64,512]{2,1,0:T(8,128)(2,1)}, u32[]{:S(2)}) copy-start(bf16[32,64,512]{2,1,0:T(8,128)(2,1)} %param.11) | copy-start | bytes 6291460
  98.6 113.8 %reduce-scatter.2.cloned.1.call-start = ((), (), s32[]{:S(2)}) async-start(), calls=%async_computation.4 | async-start | bytes 9437184 | tf_op jit(solution)/shard_map/reduce_scatter | solution.py:75
  148.2 6.2 %copy-start.4 = (f32[64,128,128]{2,1,0:T(8,128)S(1)}, f32[64,128,128]{2,1,0:T(8,128)}, u32[]{:S(2)}) copy-start(f32[64,128,128]{2,1,0:T(8,128)} %param.12) | copy-start | bytes 12582916
  236.6 8.5 %copy-start.1 = (f32[32,16,1024]{2,1,0:T(8,128)S(1)}, f32[32,16,1024]{2,1,0:T(8,128)}, u32[]{:S(2)}) copy-start(f32[32,16,1024]{2,1,0:T(8,128)} %param.8) | copy-start | bytes 6291460
  238.2 22.3 %all-to-all-start.1 = ((bf16[16,2,16384]{2,1,0:T(2,128)(2,1)}), bf16[16,2,16384]{2,1,0:T(2,128)(2,1)S(1)}, u32[]{:S(2)}, u32[]{:S(2)}) async-start(bf16[16,2,16384]{2,1,0:T(2,128)(2,1)} %reshape.816), calls=%async_computation.2 | async-start | bytes 2097152 | tf_op jit(solution)/shard_map/all_to_all | solution.py:77
  277.0 3.0 copy-start
  277.0 3.0 copy-start.2
  277.0 3.5 copy-start.6
Sparse Core Ops, SparseCore 0:
  98.7 49.4 all-gather.2
  160.7 51.6 reduce-scatter.1
